TPU v7x, 32 devices: a whole 2x2x4 slice. The times are simulated.
32 devices in a mesh: groups: 2 (over y), seq: 8 (over z, core), side: 1, req: 2 (over x).
Axes of the slice: x: 2, y: 2, z: 4, core: 2. Of those that a mesh axis runs over, the one named last changes fastest.
Arguments:
- queries: bfloat16 [4, 128, 4, 2048], P(('groups', 'req'), 'seq', 'side'), parts along dimension 0, may hold values from -8 to 8
- cache_keys: bfloat16 [4, 1024, 512], P(('groups', 'req'), 'seq', 'side'), parts along dimension 0, may hold values from -8 to 8
- cache_values: bfloat16 [4, 1024, 512], P(('groups', 'req'), 'seq', 'side'), parts along dimension 0, may hold values from -6 to 6
- tree_keys: bfloat16 [4, 128, 512], P(('groups', 'req'), 'seq', 'side'), parts along dimension 0, may hold values from -8 to 8
- tree_values: bfloat16 [4, 128, 512], P(('groups', 'req'), 'seq', 'side'), parts along dimension 0, may hold values from -6 to 6
- parents: int32 [4, 128], P(('groups', 'req')), parts along dimension 0, may hold values from 0 to 126, as said below
- lengths: int32 [4], P(('groups', 'req')), parts along dimension 0, may hold values from 128 to 1024
- out_weight: bfloat16 [4, 2048, 4096], P('side', 'seq', 'req'), may hold values from -0.0625 to 0.0625
- in_experts: bfloat16 [64, 4096, 1024], P(('seq', 'side'), 'req'), may hold values from -0.09375 to 0.09375
- out_experts: bfloat16 [64, 1024, 4096], P(('seq', 'side'), None, 'req'), may hold values from -0.1875 to 0.1875
- gate_experts: int32 [512, 8], P(('groups', 'seq', 'side')), parts along dimension 0, may hold values from 0 to 63, all different within a row; in each aligned block of 32 rows (0 to 31, 32 to 63, ...) at most 6 rows name the same one
- gate_weights: float32 [512, 8], P(('groups', 'seq', 'side')), parts along dimension 0, may hold values from 0.1 to 1
Outputs:
- attended: bfloat16 [512, 4096], P(('groups', 'seq', 'side'), 'req'), parts along dimension 0
- expert_out: bfloat16 [512, 4096], P(('groups', 'seq', 'side'), 'req'), parts along dimension 0
There are 2 independent parts, one for each index of `groups`. A program takes and returns all parts, laid end to end along the dimension named above; an argument that names none is the same for every part. Nothing has to cross between parts.
Inputs may be any that keep to these rules, and one draw needn't show every extreme that they name: parents[r, 0] is 0; every node i >= 1 has its parent among nodes i - 4 to i - 1. `gate_experts`: within the 32 rows that one device holds along seq+side, no expert is named by more than 6 rows, and in some such block one expert is named exactly 6 times.
All inputs are finite; a program needn't handle non-finite values.
Results may differ from a plain program's by a relative error of at most 0.018.
Values may be sent and summed in bfloat16 or wider, within the bound.
No kernel may reach another device: no remote copies, remote signals or barrier semaphores. Data moves between devices by JAX's collectives and lax.ppermute only.
A program may use at most 128 MiB of HBM per device.

v0:
```python
import math
import jax
import jax.numpy as jnp
from jax import lax
from jax.sharding import PartitionSpec as P

GROUP = 16
HD = 128
EXPERTS = 64
CAP = 6
NEG_FILL = -1e30


def ancestors(parent_row, node_count):
    node_ids = jnp.arange(node_count, dtype=jnp.int32)
    parent_hit = (node_ids[None, :] == parent_row[:, None]).astype(jnp.float32)
    reached = jnp.maximum(parent_hit, jnp.eye(node_count, dtype=jnp.float32))
    for turn_number in range(max(1, (node_count - 1).bit_length())):
        reached = jnp.minimum(jnp.dot(reached, reached, precision=lax.Precision.HIGHEST), 1.0)
    return reached


def per_device(
    queries,
    cache_keys,
    cache_values,
    tree_keys,
    tree_values,
    parents,
    lengths,
    out_weight,
    in_experts,
    out_experts,
    gate_experts,
    gate_weights,
):
    seq_index = lax.axis_index("seq")
    ctx_local = cache_keys.shape[1]
    nodes_local = queries.shape[1]
    kv_local = queries.shape[2]
    gathered = lax.all_gather(queries, "seq", axis=1, tiled=True)
    node_count = gathered.shape[1]
    reached = ancestors(parents[0], node_count)
    tree_seen = lax.dynamic_slice_in_dim(reached, seq_index * nodes_local, nodes_local, 1) > 0.5
    positions = seq_index * ctx_local + jnp.arange(ctx_local, dtype=jnp.int32)
    context_seen = jnp.broadcast_to((positions < lengths[0])[None, :], (node_count, ctx_local))
    visible = jnp.concatenate([context_seen, tree_seen], axis=1)[None]
    factor = 1.0 / math.sqrt(HD)
    outputs, maxima, totals = ([], [], [])
    for head_pair in range(kv_local):
        first_col = head_pair * HD
        key_rows = jnp.concatenate(
            [
                cache_keys[0, :, first_col : first_col + HD],
                tree_keys[0, :, first_col : first_col + HD],
            ],
            axis=0,
        )
        value_rows = jnp.concatenate(
            [
                cache_values[0, :, first_col : first_col + HD],
                tree_values[0, :, first_col : first_col + HD],
            ],
            axis=0,
        )
        query_block = gathered[0, :, head_pair].reshape(node_count, GROUP, HD)
        scores = (
            jnp.einsum("ngd,kd->gnk", query_block, key_rows, preferred_element_type=jnp.float32)
            * factor
        )
        masked = jnp.where(visible, scores, NEG_FILL)
        row_max = jnp.max(masked, axis=-1)
        weights = jnp.where(visible, jnp.exp(masked - row_max[..., None]), 0.0)
        weights_low = weights.astype(jnp.bfloat16)
        outputs.append(
            jnp.einsum("gnk,kd->gnd", weights_low, value_rows, preferred_element_type=jnp.float32)
        )
        maxima.append(row_max)
        totals.append(jnp.sum(weights, axis=-1))
    partial_out = jnp.stack(outputs)
    partial_max = jnp.stack(maxima)
    partial_sum = jnp.stack(totals)
    pieces = (
        lax.all_to_all(partial_out[None], "seq", split_axis=2, concat_axis=0, tiled=True),
        lax.all_to_all(partial_max[None], "seq", split_axis=2, concat_axis=0, tiled=True),
        lax.all_to_all(partial_sum[None], "seq", split_axis=2, concat_axis=0, tiled=True),
    )
    larger = jnp.max(pieces[1], axis=0)
    scales = jnp.exp(pieces[1] - larger[None])
    merged = jnp.sum(pieces[0] * scales[..., None], axis=0)
    summed = jnp.sum(pieces[2] * scales, axis=0)
    attention = merged / summed[..., None]
    attention = jnp.transpose(attention, (2, 0, 1, 3)).reshape(node_count, -1).astype(jnp.bfloat16)
    head_rows = lax.all_gather(attention, "req", axis=0, tiled=True)
    projector = out_weight.reshape(-1, out_weight.shape[2])
    attended = lax.psum_scatter(
        jnp.dot(head_rows, projector, preferred_element_type=jnp.float32),
        ("seq", "side"),
        scatter_dimension=0,
        tiled=True,
    ).astype(jnp.bfloat16)
    local_experts = in_experts.shape[0]
    flat_ids = gate_experts.reshape(-1)
    expert_hit = (flat_ids[:, None] == jnp.arange(EXPERTS, dtype=jnp.int32)[None, :]).astype(
        jnp.int32
    )
    earlier = jnp.cumsum(expert_hit, axis=0) - expert_hit
    slot_rank = jnp.sum(earlier * expert_hit, axis=1)
    slot_ids = (flat_ids * CAP + slot_rank).reshape(gate_experts.shape)
    slot_count = EXPERTS * CAP
    matches = jnp.arange(slot_count, dtype=jnp.int32)[:, None, None] == slot_ids[None]
    placing = jnp.any(matches, axis=2).astype(jnp.bfloat16)
    mixing = jnp.sum(jnp.where(matches, gate_weights[None], 0.0), axis=2)
    outgoing = jnp.dot(placing, attended, preferred_element_type=jnp.float32).astype(jnp.bfloat16)
    device_count = EXPERTS // local_experts
    outgoing = outgoing.reshape(device_count, local_experts, CAP, -1)
    before = jnp.einsum(
        "sekd,edf->sekf",
        lax.all_to_all(outgoing, ("seq", "side"), split_axis=0, concat_axis=0, tiled=True),
        in_experts,
        preferred_element_type=jnp.float32,
    )
    hidden_sum = lax.psum(before, "req")
    hidden = jax.nn.silu(hidden_sum).astype(jnp.bfloat16)
    produced = jnp.einsum(
        "sekf,efd->sekd", hidden, out_experts, preferred_element_type=jnp.float32
    ).astype(jnp.bfloat16)
    came_back = lax.all_to_all(produced, ("seq", "side"), split_axis=0, concat_axis=0, tiled=True)
    slot_rows = came_back.reshape(slot_count, -1).astype(jnp.float32)
    expert_mix = jnp.dot(mixing.T, slot_rows, precision=lax.Precision.HIGHEST)
    return (attended, expert_mix.astype(jnp.bfloat16))


def solution(mesh):
    placed = (
        P(("groups", "req"), "seq", "side", None),
        P(("groups", "req"), "seq", "side"),
        P(("groups", "req"), "seq", "side"),
        P(("groups", "req"), "seq", "side"),
        P(("groups", "req"), "seq", "side"),
        P(("groups", "req"), None),
        P(("groups", "req")),
        P("side", "seq", "req"),
        P(("seq", "side"), "req", None),
        P(("seq", "side"), None, "req"),
        P(("groups", "seq", "side"), None),
        P(("groups", "seq", "side"), None),
    )
    return jax.shard_map(
        per_device,
        mesh=mesh,
        in_specs=placed,
        out_specs=(P(("groups", "seq", "side"), "req"), P(("groups", "seq", "side"), "req")),
        check_vma=False,
    )
```

profile of v0, /device:TPU:0, one launch (start us, length us, event | category | flops | bytes accessed | tf_op | source)
XLA Modules:
  0.0 424.0 jit_solution(3540894547488860294)
XLA Ops:
  7.3 0.7 all-gather.2.cloned.1.call-update
  8.6 1.1 convolution_minimum_fusion.5
  9.7 0.2 convolution_minimum_fusion.4
  9.9 0.2 convolution_minimum_fusion.3
  10.1 0.2 convolution_minimum_fusion.2
  10.3 0.2 convolution_minimum_fusion.1
  10.6 0.2 convolution_minimum_fusion
  10.8 0.2 fusion.95
  11.1 0.6 slice_bitcast_fusion.15
  11.7 0.6 slice_bitcast_fusion.14
  12.3 0.6 slice_bitcast_fusion.7
  13.0 0.6 slice_bitcast_fusion.6
  13.6 27.9 %all-gather.2.cloned.1.call-done = bf16[1,128,4,2048]{3,2,0,1:T(4,128)(2,1)} async-done(((bf16[1,16,4,2048]{3,2,0,1:T(4,128)(2,1)}), bf16[1,128,4,2048]{3,2,0,1:T(4,128)(2,1)}) %all-gather.2.cloned.1.call-update) | async-done | bytes 2097168 | tf_op jit(solution)/shard_map/all_gather | solution.py:41
  41.6 9.0 %fusion.90 = (bf16[1,128,1,2048]{3,2,0,1:T(2,128)(2,1)S(1)}, bf16[1,128,1,2048]{3,2,0,1:T(2,128)(2,1)}, bf16[1,128,1,2048]{3,2,0,1:T(2,128)(2,1)S(1)}, bf16[1,128,1,2048]{3,2,0,1:T(2,128)(2,1)S(1)}) fusion(bf16[1,128,4,2048]{3,2,0,1:T(4,128)(2,1)} %all-gather.2.cloned.1.call-done), kind=kLoop, calls=%fused_computation.143 | loop fusion | bytes 4194304 | tf_op jit(solution)/shard_map/slice | solution.py:66
  50.5 3.5 copy.144
  54.0 1.9 copy.143
  55.9 0.8 copy.142
  56.8 1.9 copy.145
  58.7 0.3 fusion.92
  59.0 0.7 copy-done.4
  59.7 0.3 fusion.93
  60.1 0.3 fusion.94
  60.4 0.6 copy-done.3
  61.1 1.0 fusion.91
  62.1 1.1 fusion.25
  63.3 0.7 maximum_bitcast_fusion.18
  64.0 4.0 all-to-all-start.2
  68.0 2.8 convolution_bitcast_fusion.3
  70.8 1.5 convolution_bitcast_fusion.2
  72.4 1.5 convolution_bitcast_fusion.1
  73.9 1.5 convolution_bitcast_fusion
  75.4 0.7 maximum_bitcast_fusion.17
  76.0 5.0 %all-to-all-start.1 = ((f32[1,4,16,128]{3,1,0,2:T(4,128)}), f32[1,4,16,128]{3,1,0,2:T(4,128)S(1)}, u32[]{:S(2)}, u32[]{:S(2)}) async-start(f32[1,4,16,128]{3,1,0,2:T(4,128)} %maximum_bitcast_fusion.17), calls=%async_computation.1 | async-start | bytes 65536 | tf_op jit(solution)/shard_map/all_to_all | solution.py:85
  81.1 1.9 maximum_bitcast_fusion
  83.0 2.2 copy.116
  85.2 1.6 all-to-all-done.1
  86.8 4.5 %all-to-all-start = ((f32[1,4,16,128,128]{4,3,1,0,2:T(8,128)}), f32[1,4,16,128,128]{4,3,1,0,2:T(8,128)}, u32[]{:S(2)}, u32[]{:S(2)}) async-start(f32[1,4,16,128,128]{4,3,1,0,2:T(8,128)} %copy.116), calls=%async_computation | async-start | bytes 8388608 | tf_op jit(solution)/shard_map/all_to_all | solution.py:84
  91.4 0.8 multiply_reduce_fusion
  92.2 93.1 %all-to-all-done = f32[1,4,16,128,128]{4,3,1,0,2:T(8,128)} async-done(((f32[1,4,16,128,128]{4,3,1,0,2:T(8,128)}), f32[1,4,16,128,128]{4,3,1,0,2:T(8,128)}, u32[]{:S(2)}, u32[]{:S(2)}) %all-to-all-start) | async-done | bytes 4194336 | tf_op jit(solution)/shard_map/all_to_all | solution.py:84
  185.3 2.9 fusion.4
  188.2 0.2 fusion.50
  188.6 8.5 %all_gather.7 = bf16[256,1024]{0,1:T(8,128)(2,1)S(1)} all-gather(bf16[128,1024]{0,1:T(8,128)(2,1)S(1)} %bitcast.199), channel_id=1, replica_groups=mesh['groups'=2,'seq'=8,'side'=1,'req'=2] {'req'}, dimensions={0}, use_global_device_ids=true | all-gather | bytes 786432 | tf_op jit(solution)/shard_map/all_gather | solution.py:94
  197.1 4.8 %fusion.96 = f32[256,2048]{1,0:T(8,128)} fusion(bf16[256,1024]{0,1:T(8,128)(2,1)S(1)} %all_gather.7, bf16[1024,2048]{1,0:T(8,128)(2,1)} %bitcast.212), kind=kOutput, calls=%fused_computation.149 | convolution fusion | flops 1073741824 | bytes 6815744 | tf_op jit(solution)/shard_map/dot_general | solution.py:97
  201.9 0.2 all-reduce.2.cloned.1.call-start
  202.1 0.4 copy-done.26
  202.8 0.6 reduce-window.6
  203.5 0.2 slice_reduce_fusion
  203.9 0.2 fusion.51
  204.1 33.4 %reduce-scatter.2.cloned.1.call-done = f32[32,2048]{1,0:T(8,128)} async-done(((f32[256,2048]{1,0:T(8,128)}), f32[32,2048]{1,0:T(8,128)}) %reduce-scatter.2.cloned.1.call-update) | async-done | bytes 262160 | tf_op jit(solution)/shard_map/reduce_scatter | solution.py:96
  237.5 1.0 convert_element_type.59
  238.5 1.8 convolution_convert_fusion
  240.3 2.5 reshape.61
  242.8 0.9 copy.126
  243.7 40.2 %all_to_all.64 = bf16[8,8,6,2048]{3,1,2,0:T(8,128)(2,1)S(1)} all-to-all(bf16[8,8,6,2048]{3,1,2,0:T(8,128)(2,1)S(1)} %copy.126), channel_id=1, replica_groups=mesh['groups'=2,'seq'=8,'side'=1,'req'=2] {'seq','side'}, dimensions={0} | all-to-all | bytes 3145728 | tf_op jit(solution)/shard_map/all_to_all | solution.py:119
  283.9 14.8 %fusion.12 = f32[8,8,6,1024]{3,0,2,1:T(8,128)} fusion(bf16[8,2048,1024]{2,1,0:T(8,128)(2,1)} %param.20, bf16[8,8,6,2048]{3,1,2,0:T(8,128)(2,1)S(1)} %all_to_all.64), kind=kOutput, calls=%fused_computation.13 | convolution fusion | flops 1610612736 | bytes 36700160 | tf_op jit(solution)/shard_map/sekd,edf->sekf/dot_general | solution.py:117
  298.7 50.5 %all-reduce.2.cloned.1.call-done = f32[8,8,6,1024]{3,0,2,1:T(8,128)} async-done(((f32[8,8,6,1024]{3,0,2,1:T(8,128)}), f32[8,8,6,1024]{3,0,2,1:T(8,128)}) %all-reduce.2.cloned.1.call-update) | async-done | bytes 1572880 | tf_op jit(solution)/shard_map/psum | solution.py:123
  349.3 16.9 %fusion.8 = bf16[8,8,6,2048]{3,0,2,1:T(8,128)(2,1)S(1)} fusion(bf16[8,1024,2048]{2,1,0:T(8,128)(2,1)} %param.21, f32[8,8,6,1024]{3,0,2,1:T(8,128)} %all-reduce.2.cloned.1.call-done), kind=kOutput, calls=%fused_computation.9 | convolution fusion | flops 1613365248 | bytes 36700160 | tf_op jit(solution)/shard_map/sekf,efd->sekd/dot_general | solution.py:125
  366.2 2.0 copy.128
  368.2 4.7 %all-to-all-start.4 = ((bf16[8,8,6,2048]{3,1,2,0:T(8,128)(2,1)}), bf16[8,8,6,2048]{3,1,2,0:T(8,128)(2,1)}, u32[]{:S(2)}, u32[]{:S(2)}) async-start(bf16[8,8,6,2048]{3,1,2,0:T(8,128)(2,1)} %copy.128), calls=%async_computation.5 | async-start | bytes 3145728 | tf_op jit(solution)/shard_map/all_to_all | solution.py:128
  373.0 0.2 select_reduce_fusion
  373.2 37.6 %all-to-all-done.4 = bf16[8,8,6,2048]{3,1,2,0:T(8,128)(2,1)} async-done(((bf16[8,8,6,2048]{3,1,2,0:T(8,128)(2,1)}), bf16[8,8,6,2048]{3,1,2,0:T(8,128)(2,1)}, u32[]{:S(2)}, u32[]{:S(2)}) %all-to-all-start.4) | async-done | bytes 1572896 | tf_op jit(solution)/shard_map/all_to_all | solution.py:128
  410.8 2.3 copy.129
  413.1 1.5 reshape.62
  414.6 2.9 convolution_convert_fusion.1
  (76 shorter events, 1.1 us)
Async XLA Ops:
  7.2 3.9 copy-start.24
  7.2 4.5 %copy-start.25 = (bf16[1,16,512]{2,1,0:T(8,128)(2,1)S(1)}, bf16[1,16,512]{2,1,0:T(8,128)(2,1)}, u32[]{:S(2)}) copy-start(bf16[1,16,512]{2,1,0:T(8,128)(2,1)} %param.16) | copy-start | bytes 49156
  7.2 5.1 %copy-start.14 = (bf16[1,128,512]{2,1,0:T(8,128)(2,1)S(1)}, bf16[1,128,512]{2,1,0:T(8,128)(2,1)}, u32[]{:S(2)}) copy-start(bf16[1,128,512]{2,1,0:T(8,128)(2,1)} %param.13) | copy-start | bytes 393220
  7.2 5.8 %copy-start.15 = (bf16[1,128,512]{2,1,0:T(8,128)(2,1)S(1)}, bf16[1,128,512]{2,1,0:T(8,128)(2,1)}, u32[]{:S(2)}) copy-start(bf16[1,128,512]{2,1,0:T(8,128)(2,1)} %param.14) | copy-start | bytes 393220
  7.2 34.3 %all-gather.2.cloned.1.call-start = ((), (), s32[]{:S(2)}) async-start(), calls=%async_computation.6 | async-start | bytes 2359296 | tf_op jit(solution)/shard_map/all_gather | solution.py:41
  11.1 49.0 %copy-start.6 = (pred[128,144]{0,1:T(8,128)(4,1)}, pred[128,144]{0,1:T(8,128)(4,1)S(1)}, u32[]{:S(2)}) copy-start(pred[128,144]{0,1:T(8,128)(4,1)S(1)} %pad_add_fusion) | copy-start | bytes 55300
  56.8 1.9 copy-start.5
  58.7 1.0 copy-start.4
  60.0 1.0 copy-start.3
  60.0 1.0 copy-start.16
  60.0 1.0 copy-start.23
  60.4 2.9 copy-start
  60.4 2.9 copy-start.10
  60.4 1.7 copy-start.7
  62.1 1.2 copy-start.12
  64.0 12.1 %all-to-all-start.2 = ((f32[1,4,16,128]{3,1,0,2:T(4,128)}), f32[1,4,16,128]{3,1,0,2:T(4,128)}, u32[]{:S(2)}, u32[]{:S(2)}) async-start(f32[1,4,16,128]{3,1,0,2:T(4,128)} %maximum_bitcast_fusion.18), calls=%async_computation.2 | async-start | bytes 65536 | tf_op jit(solution)/shard_map/all_to_all | solution.py:86
  67.9 2.9 copy-start.8
  67.9 2.9 copy-start.19
  68.0 2.9 copy-start.22
  70.8 1.5 copy-start.18
  70.8 1.5 copy-start.21
  72.3 1.5 copy-start.13
  72.3 1.5 copy-start.17
  72.3 1.5 copy-start.20
  73.9 1.5 copy-start.11
  73.9 7.2 %copy-start.1 = (f32[1,16,128,128]{3,2,1,0:T(8,128)S(1)}, f32[1,16,128,128]{3,2,1,0:T(8,128)}, u32[]{:S(2)}) copy-start(f32[1,16,128,128]{3,2,1,0:T(8,128)} %convolution_bitcast_fusion.3) | copy-start | bytes 3145732
  73.9 7.2 %copy-start.2 = (f32[1,16,128,128]{3,2,1,0:T(8,128)S(1)}, f32[1,16,128,128]{3,2,1,0:T(8,128)}, u32[]{:S(2)}) copy-start(f32[1,16,128,128]{3,2,1,0:T(8,128)} %convolution_bitcast_fusion.2) | copy-start | bytes 3145732
  76.0 10.7 %all-to-all-start.1 = ((f32[1,4,16,128]{3,1,0,2:T(4,128)}), f32[1,4,16,128]{3,1,0,2:T(4,128)S(1)}, u32[]{:S(2)}, u32[]{:S(2)}) async-start(f32[1,4,16,128]{3,1,0,2:T(4,128)} %maximum_bitcast_fusion.17), calls=%async_computation.1 | async-start | bytes 65536 | tf_op jit(solution)/shard_map/all_to_all | solution.py:85
  86.8 98.5 %all-to-all-start = ((f32[1,4,16,128,128]{4,3,1,0,2:T(8,128)}), f32[1,4,16,128,128]{4,3,1,0,2:T(8,128)}, u32[]{:S(2)}, u32[]{:S(2)}) async-start(f32[1,4,16,128,128]{4,3,1,0,2:T(8,128)} %copy.116), calls=%async_computation | async-start | bytes 8388608 | tf_op jit(solution)/shard_map/all_to_all | solution.py:84
  91.3 146.2 %reduce-scatter.2.cloned.1.call-start = ((), (), s32[]{:S(2)}) async-start(), calls=%async_computation.7 | async-start | bytes 2359296 | tf_op jit(solution)/shard_map/reduce_scatter | solution.py:96
  201.9 0.7 copy-start.26
  201.9 147.4 %all-reduce.2.cloned.1.call-start = ((), (), s32[]{:S(2)}) async-start(), calls=%async_computation.8 | async-start | bytes 3145728 | tf_op jit(solution)/shard_map/psum | solution.py:123
  238.5 4.3 %copy-start.9 = (bf16[32,2048]{1,0:T(8,128)(2,1)}, bf16[32,2048]{1,0:T(8,128)(2,1)S(1)}, u32[]{:S(2)}) copy-start(bf16[32,2048]{1,0:T(8,128)(2,1)S(1)} %convert_element_type.59) | copy-start | bytes 393220
  368.2 4.7 %copy-start.27 = (f32[32,8]{0,1:T(8,128)S(1)}, f32[32,8]{0,1:T(8,128)}, u32[]{:S(2)}) copy-start(f32[32,8]{0,1:T(8,128)} %param.23) | copy-start | bytes 3076
  368.2 42.6 %all-to-all-start.4 = ((bf16[8,8,6,2048]{3,1,2,0:T(8,128)(2,1)}), bf16[8,8,6,2048]{3,1,2,0:T(8,128)(2,1)}, u32[]{:S(2)}, u32[]{:S(2)}) async-start(bf16[8,8,6,2048]{3,1,2,0:T(8,128)(2,1)} %copy.128), calls=%async_computation.5 | async-start | bytes 3145728 | tf_op jit(solution)/shard_map/all_to_all | solution.py:128
Sparse Core Ops, SparseCore 0:
  9.6 31.8 all-gather.1
  202.0 35.4 reduce-scatter.1
  298.8 50.3 all-reduce.1
where the time goes:
time: 425 us; the launch traced here: 424 us
  waiting for transfers between devices  245 us (58%)
  matrix products  52.8 us (12%)
  blocking collectives  48.7 us (11%)
  local copies, waits for them, and re-layouts  33.7 us (8%)
  starting transfers between devices  18.5 us (4%)
  between operations  14.9 us (4%)
  other arithmetic  10.5 us (2%)
    all_to_all x1, waiting for transfers between devices, per_device(): lax.all_to_all(partial_out[None], 'seq', split_axis=2, concat_axis=0, til...  93.1 us
    psum x1, waiting for transfers between devices, per_device(): hidden_sum = lax.psum(before, 'req')  50.5 us
    all_to_all x1, blocking collectives, per_device(): lax.all_to_all(outgoing, ('seq', 'side'), split_axis=0, concat_axis=0, ti...  40.2 us
    all_to_all x1, waiting for transfers between devices, per_device(): lax.all_to_all(produced, ('seq', 'side'), split_axis=0, concat_axis=0, ti...  37.6 us
    reduce_scatter x1, waiting for transfers between devices, per_device(): lax.psum_scatter(jnp.dot(head_rows, projector, preferred_element_type=jnp...  33.4 us
    all_gather x1, waiting for transfers between devices, per_device(): gathered = lax.all_gather(queries, 'seq', axis=1, tiled=True)  27.9 us
    dot_general x1, matrix products, per_device(): jnp.einsum('sekf,efd->sekd', hidden, out_experts, preferred_element_type=...  16.9 us
    dot_general x1, matrix products, per_device(): jnp.einsum('sekd,edf->sekf', lax.all_to_all(outgoing, ('seq', 'side'), sp...  14.8 us
  transfers between devices with their start and end apart: 7, of which 6 were waited for; matrix products, arithmetic and copies ran while one was open for 5% of the time, Pallas kernels for 0%

commit v1 on v0

--- a/solution.py
+++ b/solution.py
@@ -38,7 +38,7 @@
     ctx_local = cache_keys.shape[1]
     nodes_local = queries.shape[1]
     kv_local = queries.shape[2]
-    gathered = lax.all_gather(queries, "seq", axis=1, tiled=True)
+    gathered = jnp.concatenate(lax.all_gather(queries, axis_name="seq"), 1)
     node_count = gathered.shape[1]
     reached = ancestors(parents[0], node_count)
     tree_seen = lax.dynamic_slice_in_dim(reached, seq_index * nodes_local, nodes_local, 1) > 0.5

time: 425 us -> 410 us (0.965)
  local copies, waits for them, and re-layouts: 33.7 us -> 21.9 us
    unnamed x62 -> x63, local copies, waits for them, and re-layouts: 10.1 us -> 3.81 us
    slice x1 -> x5, local copies, waits for them, and re-layouts: 8.99 us -> 3.5 us  [per_device(): query_block = gathered[0, :, head_pair].reshape(node_count, GROUP, HD)]
  transfers between devices with their start and end apart: 7 -> 7, of which waited for: 6 -> 6; matrix products, arithmetic and copies ran while one was open for 5% -> 4% of each run, Pallas kernels for 0% -> 0%
where the time goes in v1:
time: 410 us; the launch traced here: 409 us
  waiting for transfers between devices  243 us (59%)
  matrix products  51.4 us (13%)
  blocking collectives  48.7 us (12%)
  local copies, waits for them, and re-layouts  21.9 us (5%)
  starting transfers between devices  18.5 us (5%)
  between operations  15 us (4%)
  other arithmetic  10.5 us (3%)
    all_to_all x1, waiting for transfers between devices, per_device(): lax.all_to_all(partial_out[None], 'seq', split_axis=2, concat_axis=0, til...  93.1 us
    psum x1, waiting for transfers between devices, per_device(): hidden_sum = lax.psum(before, 'req')  50.5 us
    all_to_all x1, blocking collectives, per_device(): lax.all_to_all(outgoing, ('seq', 'side'), split_axis=0, concat_axis=0, ti...  40.2 us
    all_to_all x1, waiting for transfers between devices, per_device(): lax.all_to_all(produced, ('seq', 'side'), split_axis=0, concat_axis=0, ti...  37.6 us
    reduce_scatter x1, waiting for transfers between devices, per_device(): lax.psum_scatter(jnp.dot(head_rows, projector, preferred_element_type=jnp...  33.4 us
    all_gather x1, waiting for transfers between devices, per_device(): gathered = jnp.concatenate(lax.all_gather(queries, axis_name='seq'), 1)  26.7 us
    dot_general x1, matrix products, per_device(): jnp.einsum('sekf,efd->sekd', hidden, out_experts, preferred_element_type=...  16.9 us
    dot_general x1, matrix products, per_device(): jnp.einsum('sekd,edf->sekf', lax.all_to_all(outgoing, ('seq', 'side'), sp...  14.8 us
  transfers between devices with their start and end apart: 7, of which 6 were waited for; matrix products, arithmetic and copies ran while one was open for 4% of the time, Pallas kernels for 0%

profile of v1, /device:TPU:0, one launch (start us, length us, event | category | flops | bytes accessed | tf_op | source)
XLA Modules:
  0.0 408.8 jit_solution(16134296569815156268)
XLA Ops:
  7.3 1.9 copy.125
  9.9 1.1 convolution_minimum_fusion.5
  10.9 0.2 convolution_minimum_fusion.4
  11.2 0.2 convolution_minimum_fusion.3
  11.4 0.2 convolution_minimum_fusion.2
  11.6 0.2 convolution_minimum_fusion.1
  11.8 0.2 convolution_minimum_fusion
  12.0 0.2 fusion.95
  12.4 0.6 slice_bitcast_fusion.15
  13.0 0.6 slice_bitcast_fusion.14
  13.6 0.6 slice_bitcast_fusion.7
  14.2 0.7 slice_bitcast_fusion.6
  14.9 26.7 %all-gather.3.cloned.1.call-done = bf16[8,16,4,2048]{3,1,0,2:T(8,128)(2,1)} async-done(((bf16[1,16,4,2048]{3,1,0,2:T(8,128)(2,1)}), bf16[8,16,4,2048]{3,1,0,2:T(8,128)(2,1)}) %all-gather.3.cloned.1.call-update) | async-done | bytes 2097168 | tf_op jit(solution)/shard_map/all_gather | solution.py:41
  41.5 1.7 fusion.90
  43.2 0.3 copy.130
  43.5 0.3 copy.128
  43.8 0.3 copy.126
  44.0 1.0 copy.132
  45.1 0.3 fusion.92
  45.4 0.4 copy-done.16
  45.8 1.0 fusion.93
  46.9 0.3 fusion.94
  47.3 0.6 copy-done.3
  47.9 0.3 fusion.91
  48.3 1.1 fusion.25
  49.5 0.7 maximum_bitcast_fusion.18
  50.1 4.0 all-to-all-start.2
  54.1 2.4 convolution_bitcast_fusion.2
  56.6 0.5 convolution_bitcast_fusion.3
  57.3 1.5 convolution_bitcast_fusion.1
  58.8 1.5 convolution_bitcast_fusion
  60.3 0.6 maximum_bitcast_fusion.17
  60.9 5.0 %all-to-all-start.1 = ((f32[1,4,16,128]{3,1,0,2:T(4,128)}), f32[1,4,16,128]{3,1,0,2:T(4,128)S(1)}, u32[]{:S(2)}, u32[]{:S(2)}) async-start(f32[1,4,16,128]{3,1,0,2:T(4,128)} %maximum_bitcast_fusion.17), calls=%async_computation.1 | async-start | bytes 65536 | tf_op jit(solution)/shard_map/all_to_all | solution.py:85
  65.9 1.9 maximum_bitcast_fusion
  67.8 2.2 copy.134
  70.1 1.6 all-to-all-done.1
  71.7 4.5 %all-to-all-start = ((f32[1,4,16,128,128]{4,3,1,0,2:T(8,128)}), f32[1,4,16,128,128]{4,3,1,0,2:T(8,128)}, u32[]{:S(2)}, u32[]{:S(2)}) async-start(f32[1,4,16,128,128]{4,3,1,0,2:T(8,128)} %copy.134), calls=%async_computation | async-start | bytes 8388608 | tf_op jit(solution)/shard_map/all_to_all | solution.py:84
  76.3 0.8 multiply_reduce_fusion
  77.1 93.1 %all-to-all-done = f32[1,4,16,128,128]{4,3,1,0,2:T(8,128)} async-done(((f32[1,4,16,128,128]{4,3,1,0,2:T(8,128)}), f32[1,4,16,128,128]{4,3,1,0,2:T(8,128)}, u32[]{:S(2)}, u32[]{:S(2)}) %all-to-all-start) | async-done | bytes 4194336 | tf_op jit(solution)/shard_map/all_to_all | solution.py:84
  170.2 2.9 fusion.4
  173.1 0.2 fusion.50
  173.5 8.5 %all_gather.11 = bf16[256,1024]{0,1:T(8,128)(2,1)S(1)} all-gather(bf16[128,1024]{0,1:T(8,128)(2,1)S(1)} %bitcast.200), channel_id=1, replica_groups=mesh['groups'=2,'seq'=8,'side'=1,'req'=2] {'req'}, dimensions={0}, use_global_device_ids=true | all-gather | bytes 786432 | tf_op jit(solution)/shard_map/all_gather | solution.py:94
  181.9 4.8 %fusion.96 = f32[256,2048]{1,0:T(8,128)} fusion(bf16[256,1024]{0,1:T(8,128)(2,1)S(1)} %all_gather.11, bf16[1024,2048]{1,0:T(8,128)(2,1)} %bitcast.212), kind=kOutput, calls=%fused_computation.149 | convolution fusion | flops 1073741824 | bytes 6815744 | tf_op jit(solution)/shard_map/dot_general | solution.py:97
  186.8 0.2 all-reduce.2.cloned.1.call-start
  187.0 0.4 copy-done.28
  187.7 0.6 reduce-window.6
  188.3 0.2 slice_reduce_fusion
  188.7 0.2 fusion.51
  188.9 33.4 %reduce-scatter.2.cloned.1.call-done = f32[32,2048]{1,0:T(8,128)} async-done(((f32[256,2048]{1,0:T(8,128)}), f32[32,2048]{1,0:T(8,128)}) %reduce-scatter.2.cloned.1.call-update) | async-done | bytes 262160 | tf_op jit(solution)/shard_map/reduce_scatter | solution.py:96
  222.4 1.0 convert_element_type.59
  223.3 1.8 convolution_convert_fusion
  225.1 2.5 reshape.65
  227.6 0.9 copy.144
  228.5 40.2 %all_to_all.64 = bf16[8,8,6,2048]{3,1,2,0:T(8,128)(2,1)S(1)} all-to-all(bf16[8,8,6,2048]{3,1,2,0:T(8,128)(2,1)S(1)} %copy.144), channel_id=1, replica_groups=mesh['groups'=2,'seq'=8,'side'=1,'req'=2] {'seq','side'}, dimensions={0} | all-to-all | bytes 3145728 | tf_op jit(solution)/shard_map/all_to_all | solution.py:119
  268.8 14.8 %fusion.12 = f32[8,8,6,1024]{3,0,2,1:T(8,128)} fusion(bf16[8,2048,1024]{2,1,0:T(8,128)(2,1)} %param.20, bf16[8,8,6,2048]{3,1,2,0:T(8,128)(2,1)S(1)} %all_to_all.64), kind=kOutput, calls=%fused_computation.13 | convolution fusion | flops 1610612736 | bytes 36700160 | tf_op jit(solution)/shard_map/sekd,edf->sekf/dot_general | solution.py:117
  283.6 50.5 %all-reduce.2.cloned.1.call-done = f32[8,8,6,1024]{3,0,2,1:T(8,128)} async-done(((f32[8,8,6,1024]{3,0,2,1:T(8,128)}), f32[8,8,6,1024]{3,0,2,1:T(8,128)}) %all-reduce.2.cloned.1.call-update) | async-done | bytes 1572880 | tf_op jit(solution)/shard_map/psum | solution.py:123
  334.1 16.9 %fusion.8 = bf16[8,8,6,2048]{3,0,2,1:T(8,128)(2,1)S(1)} fusion(bf16[8,1024,2048]{2,1,0:T(8,128)(2,1)} %param.21, f32[8,8,6,1024]{3,0,2,1:T(8,128)} %all-reduce.2.cloned.1.call-done), kind=kOutput, calls=%fused_computation.9 | convolution fusion | flops 1613365248 | bytes 36700160 | tf_op jit(solution)/shard_map/sekf,efd->sekd/dot_general | solution.py:125
  351.0 2.0 copy.146
  353.0 4.7 %all-to-all-start.4 = ((bf16[8,8,6,2048]{3,1,2,0:T(8,128)(2,1)}), bf16[8,8,6,2048]{3,1,2,0:T(8,128)(2,1)}, u32[]{:S(2)}, u32[]{:S(2)}) async-start(bf16[8,8,6,2048]{3,1,2,0:T(8,128)(2,1)} %copy.146), calls=%async_computation.5 | async-start | bytes 3145728 | tf_op jit(solution)/shard_map/all_to_all | solution.py:128
  357.8 0.2 select_reduce_fusion
  358.0 37.6 %all-to-all-done.4 = bf16[8,8,6,2048]{3,1,2,0:T(8,128)(2,1)} async-done(((bf16[8,8,6,2048]{3,1,2,0:T(8,128)(2,1)}), bf16[8,8,6,2048]{3,1,2,0:T(8,128)(2,1)}, u32[]{:S(2)}, u32[]{:S(2)}) %all-to-all-start.4) | async-done | bytes 1572896 | tf_op jit(solution)/shard_map/all_to_all | solution.py:128
  395.6 2.3 copy.147
  397.9 1.4 reshape.66
  399.4 2.9 convolution_convert_fusion.1
  (81 shorter events, 1.3 us)
Async XLA Ops:
  7.2 5.2 %copy-start.26 = (bf16[1,16,512]{2,1,0:T(8,128)(2,1)S(1)}, bf16[1,16,512]{2,1,0:T(8,128)(2,1)}, u32[]{:S(2)}) copy-start(bf16[1,16,512]{2,1,0:T(8,128)(2,1)} %param.15) | copy-start | bytes 49156
  7.2 5.8 %copy-start.27 = (bf16[1,16,512]{2,1,0:T(8,128)(2,1)S(1)}, bf16[1,16,512]{2,1,0:T(8,128)(2,1)}, u32[]{:S(2)}) copy-start(bf16[1,16,512]{2,1,0:T(8,128)(2,1)} %param.16) | copy-start | bytes 49156
  7.2 6.4 %copy-start.12 = (bf16[1,128,512]{2,1,0:T(8,128)(2,1)S(1)}, bf16[1,128,512]{2,1,0:T(8,128)(2,1)}, u32[]{:S(2)}) copy-start(bf16[1,128,512]{2,1,0:T(8,128)(2,1)} %param.13) | copy-start | bytes 393220
  7.2 7.0 %copy-start.13 = (bf16[1,128,512]{2,1,0:T(8,128)(2,1)S(1)}, bf16[1,128,512]{2,1,0:T(8,128)(2,1)}, u32[]{:S(2)}) copy-start(bf16[1,128,512]{2,1,0:T(8,128)(2,1)} %param.14) | copy-start | bytes 393220
  7.2 34.3 %all-gather.3.cloned.1.call-start = ((), (), s32[]{:S(2)}) async-start(), calls=%async_computation.8 | async-start | bytes 2359296 | tf_op jit(solution)/shard_map/all_gather | solution.py:41
  12.3 32.7 %copy-start.4 = (pred[128,144]{0,1:T(8,128)(4,1)}, pred[128,144]{0,1:T(8,128)(4,1)S(1)}, u32[]{:S(2)}) copy-start(pred[128,144]{0,1:T(8,128)(4,1)S(1)} %pad_add_fusion) | copy-start | bytes 55300
  45.1 0.8 copy-start.16
  45.1 0.8 copy-start.25
  45.4 1.5 copy-start.5
  45.4 1.5 copy-start.15
  45.4 1.5 copy-start.24
  46.9 1.0 copy-start.3
  46.9 1.0 copy-start.14
  46.9 1.0 copy-start.23
  47.3 2.2 copy-start
  47.3 2.2 copy-start.8
  48.3 1.2 copy-start.10
  50.1 10.8 %all-to-all-start.2 = ((f32[1,4,16,128]{3,1,0,2:T(4,128)}), f32[1,4,16,128]{3,1,0,2:T(4,128)}, u32[]{:S(2)}, u32[]{:S(2)}) async-start(f32[1,4,16,128]{3,1,0,2:T(4,128)} %maximum_bitcast_fusion.18), calls=%async_computation.2 | async-start | bytes 65536 | tf_op jit(solution)/shard_map/all_to_all | solution.py:86
  54.1 2.5 copy-start.1
  54.1 2.4 copy-start.6
  54.1 2.4 copy-start.9
  54.1 2.4 copy-start.19
  54.1 2.4 copy-start.22
  56.5 0.8 copy-start.18
  56.5 0.8 copy-start.21
  57.1 1.7 copy-start.11
  57.1 1.7 copy-start.17
  57.1 1.7 copy-start.20
  58.8 7.1 %copy-start.2 = (f32[1,16,128,128]{3,2,1,0:T(8,128)S(1)}, f32[1,16,128,128]{3,2,1,0:T(8,128)}, u32[]{:S(2)}) copy-start(f32[1,16,128,128]{3,2,1,0:T(8,128)} %convolution_bitcast_fusion.2) | copy-start | bytes 3145732
  60.9 10.7 %all-to-all-start.1 = ((f32[1,4,16,128]{3,1,0,2:T(4,128)}), f32[1,4,16,128]{3,1,0,2:T(4,128)S(1)}, u32[]{:S(2)}, u32[]{:S(2)}) async-start(f32[1,4,16,128]{3,1,0,2:T(4,128)} %maximum_bitcast_fusion.17), calls=%async_computation.1 | async-start | bytes 65536 | tf_op jit(solution)/shard_map/all_to_all | solution.py:85
  71.7 98.5 %all-to-all-start = ((f32[1,4,16,128,128]{4,3,1,0,2:T(8,128)}), f32[1,4,16,128,128]{4,3,1,0,2:T(8,128)}, u32[]{:S(2)}, u32[]{:S(2)}) async-start(f32[1,4,16,128,128]{4,3,1,0,2:T(8,128)} %copy.134), calls=%async_computation | async-start | bytes 8388608 | tf_op jit(solution)/shard_map/all_to_all | solution.py:84
  76.2 146.2 %reduce-scatter.2.cloned.1.call-start = ((), (), s32[]{:S(2)}) async-start(), calls=%async_computation.6 | async-start | bytes 2359296 | tf_op jit(solution)/shard_map/reduce_scatter | solution.py:96
  186.7 0.7 copy-start.28
  186.8 147.3 %all-reduce.2.cloned.1.call-start = ((), (), s32[]{:S(2)}) async-start(), calls=%async_computation.7 | async-start | bytes 3145728 | tf_op jit(solution)/shard_map/psum | solution.py:123
  223.3 4.3 %copy-start.7 = (bf16[32,2048]{1,0:T(8,128)(2,1)}, bf16[32,2048]{1,0:T(8,128)(2,1)S(1)}, u32[]{:S(2)}) copy-start(bf16[32,2048]{1,0:T(8,128)(2,1)S(1)} %convert_element_type.59) | copy-start | bytes 393220
  353.0 4.7 %copy-start.29 = (f32[32,8]{0,1:T(8,128)S(1)}, f32[32,8]{0,1:T(8,128)}, u32[]{:S(2)}) copy-start(f32[32,8]{0,1:T(8,128)} %param.23) | copy-start | bytes 3076
  353.0 42.6 %all-to-all-start.4 = ((bf16[8,8,6,2048]{3,1,2,0:T(8,128)(2,1)}), bf16[8,8,6,2048]{3,1,2,0:T(8,128)(2,1)}, u32[]{:S(2)}, u32[]{:S(2)}) async-start(bf16[8,8,6,2048]{3,1,2,0:T(8,128)(2,1)} %copy.146), calls=%async_computation.5 | async-start | bytes 3145728 | tf_op jit(solution)/shard_map/all_to_all | solution.py:128
Sparse Core Ops, SparseCore 0:
  9.6 31.8 all-gather.2
  186.9 35.4 reduce-scatter.1
  283.7 50.3 all-reduce.1
